TPU v7x, 256 devices: a whole 4x4x8 slice. The times are simulated.
256 devices in a mesh: strip: 64 (over y, z, core), chan: 4 (over x).
Axes of the slice: x: 4, y: 4, z: 8, core: 2. Of those that a mesh axis runs over, the one named last changes fastest.
Arguments:
- activations: bfloat16 [512, 128, 1280], P('strip', None, 'chan'), may hold values from -17 to 17
- weight: bfloat16 [9, 1280, 1280], P(None, None, 'chan'), may hold values from -0.0546875 to 0.0546875
- gamma: float32 [1280], replicated, may hold values from 0.25 to 1.75
- beta: float32 [1280], replicated, may hold values from -3 to 3
- group_map: int32 [1280], replicated, may hold values from 0 to 31, as said below
- lengths: int32 [64], P('strip'), may hold values from 1 to 8, 384 in all
- stale_edges: bfloat16 [128, 128, 1280], P('strip', None, 'chan'), may hold values from -6 to 6
- stale_mean: float32 [32], replicated, may hold values from -0.5 to 0.5
- stale_square: float32 [32], replicated, may hold values from 1 to 4
- old_mean: float32 [64, 32], P('strip'), may hold values from -0.5 to 0.5
- old_square: float32 [64, 32], P('strip'), may hold values from 0.5 to 6
Outputs:
- upsampled: bfloat16 [1024, 256, 1280], P('strip', None, 'chan')
- new_mean: float32 [32], replicated
- new_square: float32 [32], replicated
Inputs may be any that keep to these rules, and one draw needn't show every extreme that they name: `group_map`: every group has exactly 40 channels. The lengths sum to 384, and some strip uses all 8 rows.
All inputs are finite; a program needn't handle non-finite values. No bound on the sum of `lengths` on one device may be relied on, other than what follows from the above.
Results may differ from a plain program's by a relative error of at most 0.0027.
Values may be sent and summed in bfloat16 or wider, within the bound.
A program may use at most 64 MiB of HBM per device.

v0:
```python
import jax
import jax.numpy as jnp
from jax import lax
from jax.sharding import PartitionSpec as P

EPS = 1e-05


def from_everyone(value, axis):
    copies = jnp.broadcast_to(value, (lax.axis_size(axis), *value.shape))
    return lax.all_to_all(copies, axis, split_axis=0, concat_axis=0, tiled=True)


def over_copies(value, axis):
    return from_everyone(value, axis).sum(axis=0)


def together(arrays, axis):
    ends = [0]
    for a in arrays:
        ends.append(ends[-1] + a.size)
    subtotal = over_copies(jnp.concatenate([a.ravel() for a in arrays]), axis)
    return tuple((subtotal[b:e].reshape(a.shape) for a, b, e in zip(arrays, ends, ends[1:])))


def padded_2(block, sides, width):
    for axis, dim in sides:
        count = lax.axis_size(axis)
        forward = [(i, i + 1) for i in range(count - 1)]
        backward = [(target, source) for source, target in forward]
        low = lax.ppermute(
            lax.slice_in_dim(block, block.shape[dim] - width, None, axis=dim), axis, forward
        )
        high = lax.ppermute(lax.slice_in_dim(block, 0, width, axis=dim), axis, backward)
        block = jnp.concatenate([low, block, high], axis=dim)
    return block


def per_device(
    activations,
    weight,
    gamma,
    beta,
    group_map,
    lengths,
    stale_edges,
    stale_mean,
    stale_square,
    old_mean,
    old_square,
):
    rows, width, local_c = activations.shape
    channels = weight.shape[1]
    groups = stale_mean.shape[0]
    per_group = channels // groups
    offset = lax.axis_index("chan") * local_c
    member = (group_map[:, None] == jnp.arange(groups, dtype=jnp.int32)[None, :]).astype(
        jnp.float32
    )
    local_member = lax.dynamic_slice_in_dim(member, offset, local_c, 0)
    length = lengths[0]
    used = (jnp.arange(rows, dtype=jnp.int32) < length).astype(jnp.float32)[:, None, None]
    values = activations.astype(jnp.float32) * used
    chan_sum = jnp.sum(values, axis=(0, 1))
    chan_sq = jnp.sum(values * values, axis=(0, 1))
    part_one = jnp.sum(chan_sum[:, None] * local_member, axis=0)
    part_two = jnp.sum(chan_sq[:, None] * local_member, axis=0)
    strip_one, strip_two = together((part_one, part_two), "chan")
    total_count = float(lax.axis_size("strip") * (3 * rows // 4) * width * per_group)
    image_one, image_two = together((strip_one, strip_two), "strip")
    new_mean = image_one / total_count
    new_square = image_two / total_count
    count = length.astype(jnp.float32) * (width * per_group)
    fresh_mean = strip_one / count
    fresh_square = strip_two / count
    mean_g = stale_mean + fresh_mean - old_mean[0]
    square_g = stale_square + fresh_square - old_square[0]
    var_g = jnp.maximum(square_g - mean_g * mean_g, 0.5 * (fresh_square - fresh_mean * fresh_mean))
    rstd_g = lax.rsqrt(var_g + EPS)
    scale_c = jnp.sum(member * rstd_g[None, :], axis=1) * gamma
    shift_c = beta - jnp.sum(member * mean_g[None, :], axis=1) * scale_c
    bordered = padded_2(stale_edges, (("strip", 0),), 1)
    bounds = jnp.stack([bordered[0], bordered[3]], axis=0)
    initial = jnp.zeros((rows * width, local_c), jnp.float32)
    total = initial
    piece = lax.all_gather(activations, "chan", axis=2, tiled=True)
    bound = lax.all_gather(bounds, "chan", axis=2, tiled=True)
    depth = piece.shape[2]
    act = (jax.nn.silu(piece.astype(jnp.float32) * scale_c + shift_c) * used).astype(jnp.bfloat16)
    padded = jnp.concatenate([bound[0:1], act, jnp.zeros((1, width, depth), jnp.bfloat16)], axis=0)
    place = (jnp.arange(rows + 2, dtype=jnp.int32) == length + 1)[:, None, None]
    padded = jnp.where(place, bound[1][None], padded)
    padded = jnp.pad(padded, ((0, 0), (1, 1), (0, 0)))
    for tap in range(9):
        down, across = (tap // 3, tap % 3)
        patch = padded[down : down + rows, across : across + width].reshape(rows * width, depth)
        total = total + jnp.dot(patch, weight[tap], preferred_element_type=jnp.float32)
    block = ((activations.astype(jnp.float32) + total.reshape(rows, width, local_c)) * used).astype(
        jnp.bfloat16
    )
    upsampled = jnp.repeat(jnp.repeat(block, 2, axis=0), 2, axis=1)
    return (upsampled, new_mean, new_square)


def solution(mesh):
    in_specs = (
        P("strip", None, "chan"),
        P(None, None, "chan"),
        P(),
        P(),
        P(),
        P("strip"),
        P("strip", None, "chan"),
        P(),
        P(),
        P("strip", None),
        P("strip", None),
    )
    out_specs = (P("strip", None, "chan"), P(), P())
    return jax.shard_map(
        per_device, mesh=mesh, in_specs=in_specs, out_specs=out_specs, check_vma=False
    )
```

profile of v0, /device:TPU:2, one launch (start us, length us, event | category | flops | bytes accessed | tf_op | source)
XLA Modules:
  0.0 105.8 jit_solution(1750470864157832420)
XLA Ops:
  7.2 0.0 all-gather.2.cloned.1.call-start
  7.3 2.4 %copy.58 = bf16[8,128,320]{1,0,2:T(8,128)(2,1)} copy(bf16[8,128,320]{1,2,0:T(8,128)(2,1)} %param.11) | data formatting | bytes 1310720 | tf_op args[0]
  9.7 0.0 all-gather.2.cloned.1.call-update
  10.4 1.4 %fusion.1 = (f32[320]{0:T(512)S(1)}, f32[320]{0:T(512)S(1)}) fusion(bf16[8,128,320]{1,2,0:T(8,128)(2,1)} %param.11, f32[8]{0:T(128)S(1)} %compare_convert_fusion), kind=kLoop, calls=%fused_computation.11 | loop fusion | flops 1637760 | bytes 657952 | tf_op jit(solution)/shard_map/reduce_sum | solution.py:64
  11.9 0.2 fusion.26
  12.1 0.1 pad_maximum_fusion.1
  12.2 0.6 broadcast_in_dim.46
  12.7 5.4 %all-to-all-start = ((f32[4,1,64]{2,1,0:T(1,128)}), f32[4,1,64]{2,1,0:T(1,128)S(1)}, u32[]{:S(2)}, u32[]{:S(2)}) async-start(f32[4,1,64]{2,1,0:T(1,128)} %broadcast_in_dim.46), calls=%async_computation | async-start | bytes 4096 | tf_op jit(solution)/shard_map/all_to_all | solution.py:11
  18.2 0.1 copy.65
  18.3 1.3 %collective-permute-start = (bf16[1,128,320]{1,0,2:T(2,128)(2,1)S(1)}, bf16[1,128,320]{1,0,2:T(2,128)(2,1)S(1)}, u32[]{:S(2)}, u32[]{:S(2)}) collective-permute-start(bf16[1,128,320]{1,0,2:T(2,128)(2,1)S(1)} %copy.65), channel_id=1, source_target_pairs={{0,4},{4,8},{8,12},{12,16},{16,20},{20,24},{24,28},{28,32},{32,36}... | collective-permute-start | bytes 245768 | tf_op jit(solution)/shard_map/ppermute | solution.py:31
  19.6 0.1 copy.66
  19.8 1.3 %collective-permute-start.1 = (bf16[1,128,320]{1,0,2:T(2,128)(2,1)S(1)}, bf16[1,128,320]{1,0,2:T(2,128)(2,1)S(1)}, u32[]{:S(2)}, u32[]{:S(2)}) collective-permute-start(bf16[1,128,320]{1,0,2:T(2,128)(2,1)S(1)} %copy.66), channel_id=1, source_target_pairs={{4,0},{8,4},{12,8},{16,12},{20,16},{24,20},{28,24},{32,28},{36,32}... | collective-permute-start | bytes 245768 | tf_op jit(solution)/shard_map/ppermute | solution.py:34
  21.1 0.1 pad.7.clone
  21.2 0.8 all-to-all-done
  22.0 0.6 broadcast_in_dim.50
  22.7 14.8 %all-to-all-start.1 = ((f32[64,1,64]{2,1,0:T(1,128)}), f32[64,1,64]{2,1,0:T(1,128)S(1)}, u32[]{:S(2)}, u32[]{:S(2)}) async-start(f32[64,1,64]{2,1,0:T(1,128)} %broadcast_in_dim.50), calls=%async_computation.1 | async-start | bytes 65536 | tf_op jit(solution)/shard_map/all_to_all | solution.py:11
  37.5 0.1 add_rsqrt_fusion
  37.6 0.1 select_reduce_fusion.1
  37.8 9.2 %all-to-all-done.1 = f32[64,1,64]{2,1,0:T(1,128)S(1)} async-done(((f32[64,1,64]{2,1,0:T(1,128)}), f32[64,1,64]{2,1,0:T(1,128)S(1)}, u32[]{:S(2)}, u32[]{:S(2)}) %all-to-all-start.1) | async-done | bytes 16416 | tf_op jit(solution)/shard_map/all_to_all | solution.py:11
  47.1 0.6 slice_multiply_fusion
  47.6 0.4 pad_maximum_fusion
  48.0 13.7 %all_gather.6 = bf16[2,128,1280]{1,0,2:T(2,128)(2,1)S(1)} all-gather(bf16[2,128,320]{1,0,2:T(2,128)(2,1)S(1)} %pad_maximum_fusion), channel_id=1, replica_groups=mesh['strip'=64,'chan'=4] {'chan'}, dimensions={2}, use_global_device_ids=true | all-gather | bytes 819200 | tf_op jit(solution)/shard_map/all_gather | solution.py:87
  61.7 0.9 fusion.29
  62.6 0.5 copy.67
  63.1 0.5 copy.68
  63.5 0.0 all-gather.2.cloned.1.call-done
  63.6 3.8 %copy.59 = bf16[8,128,1280]{2,1,0:T(8,128)(2,1)S(1)} copy(bf16[8,128,1280]{1,0,2:T(8,128)(2,1)} %all-gather.2.cloned.1.call-done) | data formatting | bytes 5242880 | tf_op jit(solution)/shard_map/all_gather | solution.py:86
  67.4 1.7 %multiply_convert_fusion = bf16[8,128,1280]{2,1,0:T(8,128)(2,1)S(1)} fusion(bf16[8,128,1280]{2,1,0:T(8,128)(2,1)S(1)} %copy.59, f32[8]{0:T(128)S(1)} %compare_convert_fusion, f32[1280]{0:T(1024)S(1)} %get-tuple-element.27, f32[1280]{0:T(1024)S(1)} %get-tuple-element.28), kind=kLoop, calls=%fused_computation | loop fusion | flops 11796480 | bytes 5253152 | tf_op jit(solution)/shard_map/convert_element_type | solution.py:89
  69.1 0.5 maximum_select_fusion
  69.5 10.1 %pad_slice_fusion = (bf16[8,128,1280]{2,1,0:T(8,128)(2,1)S(1)}, bf16[8,128,1280]{2,1,0:T(8,128)(2,1)S(1)}, bf16[8,128,1280]{2,1,0:T(8,128)(2,1)S(1)}, bf16[8,128...) fusion(bf16[10,128,1280]{2,1,0:T(8,128)(2,1)S(1)} %maximum_sele, ...), kind=kLoop, calls=%fused_computation.2 | loop fusion | bytes 34734080 | tf_op jit(solution)/shard_map/slice | solution.py:96
  79.6 0.0 slice-start
  79.6 2.3 %fusion.14 = f32[1024,320]{0,1:T(8,128)S(1)} fusion(bf16[1024,1280]{1,0:T(8,128)(2,1)S(1)} %bitcast.80, bf16[9,1280,320]{1,2,0:T(8,128)(2,1)} %param.12), kind=kOutput, calls=%fused_computation.32 | convolution fusion | flops 838860800 | bytes 4751360 | tf_op jit(solution)/shard_map/dot_general | solution.py:97
  82.0 0.0 slice-start.1
  82.0 2.4 %convolution_add_fusion.7 = f32[1024,320]{0,1:T(8,128)S(1)} fusion(f32[1024,320]{0,1:T(8,128)S(1)} %fusion.14, bf16[1024,1280]{1,0:T(8,128)(2,1)S(1)} %bitcast.79, bf16[9,1280,320]{1,2,0:T(8,128)(2,1)} %param.12), kind=kOutput, calls=%fused_computation.20 | convolution fusion | flops 839188480 | bytes 6062080 | tf_op jit(solution)/shard_map/dot_general | solution.py:97
  84.4 1.1 convolution_add_fusion.6
  85.4 1.1 convolution_add_fusion.5
  86.5 1.1 convolution_add_fusion.4
  87.5 1.1 convolution_add_fusion.3
  88.6 1.1 convolution_add_fusion.2
  89.7 1.1 convolution_add_fusion.1
  90.7 0.0 copy-start
  90.7 1.1 fusion.2
  91.8 0.0 copy-done
  91.8 0.2 fusion.5
  92.0 0.2 broadcast_in_dim.48
  92.3 1.9 %copy.62 = bf16[16,128,320]{2,0,1:T(8,128)(2,1)} copy(bf16[16,128,320]{1,2,0:T(8,128)(2,1)S(1)} %bitcast.71) | data formatting | bytes 2621440 | tf_op jit(solution)/shard_map/reshape | solution.py:101
  94.2 1.7 %broadcast_in_dim.49 = bf16[16,128,2,320]{3,0,2,1:T(8,128)(2,1)S(1)} broadcast(bf16[16,128,320]{2,0,1:T(8,128)(2,1)} %copy.62), dimensions={0,1,3} | broadcast | bytes 3932160 | tf_op jit(solution)/shard_map/broadcast_in_dim | solution.py:101
  95.8 3.1 %copy.64 = bf16[16,256,320]{1,2,0:T(8,128)(2,1)} copy(bf16[16,256,320]{2,0,1:T(8,128)(2,1)S(1)} %bitcast.70) | data formatting | bytes 5242880
  (28 shorter events, 0.1 us)
Async XLA Ops:
  7.2 4.7 %copy-start.2 = (s32[1280]{0:T(1024)S(1)}, s32[1280]{0:T(1024)}, u32[]{:S(2)}) copy-start(s32[1280]{0:T(1024)} %param.15) | copy-start | bytes 15364
  7.2 11.0 %copy-start.1 = (bf16[2,128,320]{1,2,0:T(8,128)(2,1)S(1)}, bf16[2,128,320]{1,2,0:T(8,128)(2,1)}, u32[]{:S(2)}) copy-start(bf16[2,128,320]{1,2,0:T(8,128)(2,1)} %param.17) | copy-start | bytes 491524
  7.2 30.3 %copy-start.8 = (f32[32]{0:T(128)S(1)}, f32[32]{0:T(128)}, u32[]{:S(2)}) copy-start(f32[32]{0:T(128)} %param.18) | copy-start | bytes 388
  7.2 30.3 %copy-start.6 = (f32[32]{0:T(128)S(1)}, f32[32]{0:T(128)}, u32[]{:S(2)}) copy-start(f32[32]{0:T(128)} %param.19) | copy-start | bytes 388
  7.2 30.3 %copy-start.7 = (f32[1,32]{1,0:T(1,128)S(1)}, f32[1,32]{1,0:T(1,128)}, u32[]{:S(2)}) copy-start(f32[1,32]{1,0:T(1,128)} %param.20) | copy-start | bytes 388
  7.2 30.3 %copy-start.5 = (f32[1,32]{1,0:T(1,128)S(1)}, f32[1,32]{1,0:T(1,128)}, u32[]{:S(2)}) copy-start(f32[1,32]{1,0:T(1,128)} %param.21) | copy-start | bytes 388
  7.2 30.5 %copy-start.4 = (f32[1280]{0:T(1024)S(1)}, f32[1280]{0:T(1024)}, u32[]{:S(2)}) copy-start(f32[1280]{0:T(1024)} %param.13) | copy-start | bytes 15364
  7.2 30.5 %copy-start.3 = (f32[1280]{0:T(1024)S(1)}, f32[1280]{0:T(1024)}, u32[]{:S(2)}) copy-start(f32[1280]{0:T(1024)} %param.14) | copy-start | bytes 15364
  7.2 56.3 %all-gather.2.cloned.1.call-start = ((), (), s32[]{:S(2)}) async-start(), calls=%async_computation.2 | async-start | bytes 3276800 | tf_op jit(solution)/shard_map/all_gather | solution.py:86
  12.7 9.3 %all-to-all-start = ((f32[4,1,64]{2,1,0:T(1,128)}), f32[4,1,64]{2,1,0:T(1,128)S(1)}, u32[]{:S(2)}, u32[]{:S(2)}) async-start(f32[4,1,64]{2,1,0:T(1,128)} %broadcast_in_dim.46), calls=%async_computation | async-start | bytes 4096 | tf_op jit(solution)/shard_map/all_to_all | solution.py:11
  18.3 29.3 %collective-permute-start = (bf16[1,128,320]{1,0,2:T(2,128)(2,1)S(1)}, bf16[1,128,320]{1,0,2:T(2,128)(2,1)S(1)}, u32[]{:S(2)}, u32[]{:S(2)}) collective-permute-start(bf16[1,128,320]{1,0,2:T(2,128)(2,1)S(1)} %copy.65), channel_id=1, source_target_pairs={{0,4},{4,8},{8,12},{12,16},{16,20},{20,24},{24,28},{28,32},{32,36}... | collective-permute-start | bytes 245768 | tf_op jit(solution)/shard_map/ppermute | solution.py:31
  19.8 27.9 %collective-permute-start.1 = (bf16[1,128,320]{1,0,2:T(2,128)(2,1)S(1)}, bf16[1,128,320]{1,0,2:T(2,128)(2,1)S(1)}, u32[]{:S(2)}, u32[]{:S(2)}) collective-permute-start(bf16[1,128,320]{1,0,2:T(2,128)(2,1)S(1)} %copy.66), channel_id=1, source_target_pairs={{4,0},{8,4},{12,8},{16,12},{20,16},{24,20},{28,24},{32,28},{36,32}... | collective-permute-start | bytes 245768 | tf_op jit(solution)/shard_map/ppermute | solution.py:34
  22.7 24.4 %all-to-all-start.1 = ((f32[64,1,64]{2,1,0:T(1,128)}), f32[64,1,64]{2,1,0:T(1,128)S(1)}, u32[]{:S(2)}, u32[]{:S(2)}) async-start(f32[64,1,64]{2,1,0:T(1,128)} %broadcast_in_dim.50), calls=%async_computation.1 | async-start | bytes 65536 | tf_op jit(solution)/shard_map/all_to_all | solution.py:11
  79.6 4.7 %slice-start = ((s8[7372800]{0:T(1024)(128)(4,1)}), s8[4194304]{0:T(1024)(128)(4,1)S(1)}, s32[]{:S(2)}) async-start(s8[7372800]{0:T(1024)(128)(4,1)} %bitcast.84), calls=%async_computation.3 | async-start | bytes 8388608
  82.0 2.4 %slice-start.1 = ((s8[7372800]{0:T(1024)(128)(4,1)}), s8[3178496]{0:T(1024)(128)(4,1)S(1)}, s32[]{:S(2)}) async-start(s8[7372800]{0:T(1024)(128)(4,1)} %bitcast.84), calls=%async_computation.4 | async-start | bytes 6356992
  90.7 1.1 %copy-start = (bf16[8,128,320]{1,2,0:T(8,128)(2,1)S(1)}, bf16[8,128,320]{1,2,0:T(8,128)(2,1)}, u32[]{:S(2)}) copy-start(bf16[8,128,320]{1,2,0:T(8,128)(2,1)} %param.11) | copy-start | bytes 1966084
Sparse Core Ops, SparseCore 0:
  10.4 39.7 all-gather.1
where the time goes:
time: 106 us
  local copies, waits for them, and re-layouts  26.7 us (25%)
  starting transfers between devices  22.9 us (22%)
  between operations  15.1 us (14%)
  blocking collectives  13.7 us (13%)
  matrix products  12.1 us (11%)
  waiting for transfers between devices  10.1 us (10%)
  other arithmetic  5.3 us (5%)
    all_to_all x2, starting transfers between devices, from_everyone(): return lax.all_to_all(copies, axis, split_axis=0, concat_axis=0, tiled=True)  20.3 us
    all_gather x1, blocking collectives, per_device(): bound = lax.all_gather(bounds, 'chan', axis=2, tiled=True)  13.7 us
    dot_general x9, matrix products, per_device(): jnp.dot(patch, weight[tap], preferred_element_type=jnp.float32)  12.1 us
    all_to_all x2, waiting for transfers between devices, from_everyone(): return lax.all_to_all(copies, axis, split_axis=0, concat_axis=0, tiled=True)  10.1 us
    slice x1, local copies, waits for them, and re-layouts, per_device(): padded[down:down + rows, across:across + width].reshape(rows * width, depth)  10.1 us
    unnamed x28, local copies, waits for them, and re-layouts  6.78 us
    all_gather x1, local copies, waits for them, and re-layouts, per_device(): piece = lax.all_gather(activations, 'chan', axis=2, tiled=True)  3.83 us
  transfers between devices with their start and end apart: 5, of which 2 were waited for; matrix products, arithmetic and copies ran while one was open for 6% of the time, Pallas kernels for 0%

commit v1 on v0

--- a/solution.py
+++ b/solution.py
@@ -4,6 +4,23 @@
 from jax.sharding import PartitionSpec as P
 
 EPS = 1e-05
+
+
+def in_order(tiles, dim):
+    lengths = list(tiles.shape[1:])
+    lengths[dim] *= tiles.shape[0]
+    return jnp.moveaxis(tiles, 0, dim).reshape(lengths)
+
+
+def grow_blocks(value, axis):
+    size, mine = (lax.axis_size(axis), lax.axis_index(axis))
+    tiles, bit = (value[None], 1)
+    while bit < size:
+        other = lax.ppermute(tiles, axis, [(i, i ^ bit) for i in range(size)])
+        low = mine & bit == 0
+        tiles = jnp.concatenate([jnp.where(low, tiles, other), jnp.where(low, other, tiles)])
+        bit *= 2
+    return tiles
 
 
 def from_everyone(value, axis):
@@ -84,7 +101,7 @@
     initial = jnp.zeros((rows * width, local_c), jnp.float32)
     total = initial
     piece = lax.all_gather(activations, "chan", axis=2, tiled=True)
-    bound = lax.all_gather(bounds, "chan", axis=2, tiled=True)
+    bound = in_order(grow_blocks(bounds, "chan"), 2)
     depth = piece.shape[2]
     act = (jax.nn.silu(piece.astype(jnp.float32) * scale_c + shift_c) * used).astype(jnp.bfloat16)
     padded = jnp.concatenate([bound[0:1], act, jnp.zeros((1, width, depth), jnp.bfloat16)], axis=0)

time: 106 us -> 106 us (level); the launches traced: 106 us -> 104 us
  blocking collectives: 13.7 us -> 0 us
  waiting for transfers between devices: 10.1 us -> 21.6 us
  starting transfers between devices: 22.9 us -> 24.9 us
  local copies, waits for them, and re-layouts: 26.7 us -> 25.3 us
    ppermute x0 -> x2, waiting for transfers between devices: none -> 20.5 us  [grow_blocks(): other = lax.ppermute(tiles, axis, [(i, i ^ bit) for i in range(size)])]
    all_gather x1 -> x0, blocking collectives: 13.7 us -> none  [per_device(): bound = lax.all_gather(bounds, 'chan', axis=2, tiled=True)]
    all_to_all x2, waiting for transfers between devices: 10.1 us -> 1.11 us  [from_everyone(): return lax.all_to_all(copies, axis, split_axis=0, concat_axis=0, tiled=True)]
    ppermute x0 -> x2, starting transfers between devices: none -> 2.25 us  [grow_blocks(): other = lax.ppermute(tiles, axis, [(i, i ^ bit) for i in range(size)])]
    unnamed x28 -> x24, local copies, waits for them, and re-layouts: 6.78 us -> 5.69 us
  transfers between devices with their start and end apart: 5 -> 7, of which waited for: 2 -> 3; matrix products, arithmetic and copies ran while one was open for 6% -> 4% of each run, Pallas kernels for 0% -> 0%
where the time goes in v1:
time: 106 us; the launch traced here: 104 us
  local copies, waits for them, and re-layouts  25.3 us (24%)
  starting transfers between devices  24.9 us (23%)
  waiting for transfers between devices  21.6 us (20%)
  between operations  15.1 us (14%)
  matrix products  12 us (11%)
  other arithmetic  5.09 us (5%)
    ppermute x2, waiting for transfers between devices, grow_blocks(): other = lax.ppermute(tiles, axis, [(i, i ^ bit) for i in range(size)])  20.5 us
    all_to_all x2, starting transfers between devices, from_everyone(): return lax.all_to_all(copies, axis, split_axis=0, concat_axis=0, tiled=True)  20 us
    dot_general x9, matrix products, per_device(): jnp.dot(patch, weight[tap], preferred_element_type=jnp.float32)  12 us
    slice x1, local copies, waits for them, and re-layouts, per_device(): padded[down:down + rows, across:across + width].reshape(rows * width, depth)  10 us
    unnamed x24, local copies, waits for them, and re-layouts  5.69 us
    all_gather x1, local copies, waits for them, and re-layouts, per_device(): piece = lax.all_gather(activations, 'chan', axis=2, tiled=True)  4.01 us
    ppermute x2, starting transfers between devices, grow_blocks(): other = lax.ppermute(tiles, axis, [(i, i ^ bit) for i in range(size)])  2.25 us
  transfers between devices with their start and end apart: 7, of which 3 were waited for; matrix products, arithmetic and copies ran while one was open for 4% of the time, Pallas kernels for 0%

profile of v1, /device:TPU:2, one launch (start us, length us, event | category | flops | bytes accessed | tf_op | source)
XLA Modules:
  0.0 104.0 jit_solution(6800328070437602725)
XLA Ops:
  7.2 0.0 all-gather.2.cloned.1.call-start
  7.3 2.4 %copy.42 = bf16[8,128,320]{1,0,2:T(8,128)(2,1)} copy(bf16[8,128,320]{1,2,0:T(8,128)(2,1)} %param.11) | data formatting | bytes 1310720 | tf_op args[0]
  9.7 0.0 all-gather.2.cloned.1.call-update
  10.4 1.4 %fusion.1 = (f32[320]{0:T(512)S(1)}, f32[320]{0:T(512)S(1)}) fusion(bf16[8,128,320]{1,2,0:T(8,128)(2,1)} %param.11, f32[8]{0:T(128)S(1)} %compare_convert_fusion), kind=kLoop, calls=%fused_computation.11 | loop fusion | flops 1637760 | bytes 657952 | tf_op jit(solution)/shard_map/reduce_sum | solution.py:81
  11.9 0.2 fusion.26
  12.1 0.1 pad_maximum_fusion.1
  12.2 0.6 broadcast_in_dim.50
  12.8 5.4 %all-to-all-start = ((f32[4,1,64]{2,1,0:T(1,128)}), f32[4,1,64]{2,1,0:T(1,128)S(1)}, u32[]{:S(2)}, u32[]{:S(2)}) async-start(f32[4,1,64]{2,1,0:T(1,128)} %broadcast_in_dim.50), calls=%async_computation | async-start | bytes 4096 | tf_op jit(solution)/shard_map/all_to_all | solution.py:28
  18.2 1.3 %collective-permute-start = (bf16[1,128,320]{1,2,0:T(8,128)(2,1)S(1)}, bf16[1,128,320]{1,2,0:T(8,128)(2,1)S(1)}, u32[]{:S(2)}, u32[]{:S(2)}) collective-permute-start(bf16[1,128,320]{1,2,0:T(8,128)(2,1)S(1)} %get-tuple-element.43), channel_id=1, source_target_pairs={{0,4},{4,8},{8,12},{12,16},{16,20},{20,24},{24,28},{28,32},{32,36}... | collective-permute-start | bytes 245768 | tf_op jit(solution)/shard_map/ppermute | solution.py:48
  19.5 1.3 %collective-permute-start.1 = (bf16[1,128,320]{1,2,0:T(8,128)(2,1)S(1)}, bf16[1,128,320]{1,2,0:T(8,128)(2,1)S(1)}, u32[]{:S(2)}, u32[]{:S(2)}) collective-permute-start(bf16[1,128,320]{1,2,0:T(8,128)(2,1)S(1)} %get-tuple-element.44), channel_id=1, source_target_pairs={{4,0},{8,4},{12,8},{16,12},{20,16},{24,20},{28,24},{32,28},{36,32}... | collective-permute-start | bytes 245768 | tf_op jit(solution)/shard_map/ppermute | solution.py:51
  20.8 0.1 pad.7.clone
  20.9 1.1 %all-to-all-done = f32[4,1,64]{2,1,0:T(1,128)S(1)} async-done(((f32[4,1,64]{2,1,0:T(1,128)}), f32[4,1,64]{2,1,0:T(1,128)S(1)}, u32[]{:S(2)}, u32[]{:S(2)}) %all-to-all-start) | async-done | bytes 1056 | tf_op jit(solution)/shard_map/all_to_all | solution.py:28
  22.0 0.6 broadcast_in_dim.54
  22.7 14.6 %all-to-all-start.1 = ((f32[64,1,64]{2,1,0:T(1,128)}), f32[64,1,64]{2,1,0:T(1,128)S(1)}, u32[]{:S(2)}, u32[]{:S(2)}) async-start(f32[64,1,64]{2,1,0:T(1,128)} %broadcast_in_dim.54), calls=%async_computation.1 | async-start | bytes 65536 | tf_op jit(solution)/shard_map/all_to_all | solution.py:28
  37.3 0.1 collective-permute-start.2
  37.5 0.1 add_rsqrt_fusion
  37.5 0.1 select_reduce_fusion.1
  37.7 10.1 %collective-permute-done.2 = bf16[1,2,128,320]{2,3,0,1:T(8,128)(2,1)S(1)} collective-permute-done((bf16[1,2,128,320]{2,3,0,1:T(8,128)(2,1)S(1)}, bf16[1,2,128,320]{2,3,0,1:T(8,128)(2,1)S(1)}, u32[]{:S(2)}, u32[]{:S(2)}) %collective-permute-start.2) | collective-permute-done | bytes 163872 | tf_op jit(solution)/shard_map/ppermute | solution.py:19
  47.8 2.2 %collective-permute-start.3 = (bf16[2,2,128,320]{2,3,0,1:T(8,128)(2,1)S(1)}, bf16[2,2,128,320]{2,3,0,1:T(8,128)(2,1)S(1)}, u32[]{:S(2)}, u32[]{:S(2)}) collective-permute-start(bf16[2,2,128,320]{2,3,0,1:T(8,128)(2,1)S(1)} %pad_maximum_fusion), channel_id=1, source_target_pairs={{0,2},{1,3},{2,0},{3,1},{4,6},{5,7},{6,4},{7,5},{8,10},{9,11},{10,... | collective-permute-start | bytes 983048 | tf_op jit(solution)/shard_map/ppermute | solution.py:19
  50.0 0.6 slice_multiply_fusion
  50.6 10.4 %collective-permute-done.3 = bf16[2,2,128,320]{2,3,0,1:T(8,128)(2,1)S(1)} collective-permute-done((bf16[2,2,128,320]{2,3,0,1:T(8,128)(2,1)S(1)}, bf16[2,2,128,320]{2,3,0,1:T(8,128)(2,1)S(1)}, u32[]{:S(2)}, u32[]{:S(2)}) %collective-permute-start.3) | collective-permute-done | bytes 327712 | tf_op jit(solution)/shard_map/ppermute | solution.py:19
  61.1 0.1 maximum_bitcast_fusion
  61.2 0.2 copy.41
  61.4 0.2 copy.45
  61.6 0.0 all-gather.2.cloned.1.call-done
  61.6 4.0 %copy.43 = bf16[8,128,1280]{2,1,0:T(8,128)(2,1)S(1)} copy(bf16[8,128,1280]{1,0,2:T(8,128)(2,1)} %all-gather.2.cloned.1.call-done) | data formatting | bytes 5242880 | tf_op jit(solution)/shard_map/all_gather | solution.py:103
  65.6 1.7 %multiply_convert_fusion = bf16[8,128,1280]{2,1,0:T(8,128)(2,1)S(1)} fusion(bf16[8,128,1280]{2,1,0:T(8,128)(2,1)S(1)} %copy.43, f32[8]{0:T(128)S(1)} %compare_convert_fusion, f32[1280]{0:T(1024)S(1)} %get-tuple-element.24, f32[1280]{0:T(1024)S(1)} %get-tuple-element.25), kind=kLoop, calls=%fused_computation | loop fusion | flops 11796480 | bytes 5253152 | tf_op jit(solution)/shard_map/convert_element_type | solution.py:106
  67.3 0.4 maximum_select_fusion
  67.7 10.0 %pad_slice_fusion = (bf16[8,128,1280]{2,1,0:T(8,128)(2,1)S(1)}, bf16[8,128,1280]{2,1,0:T(8,128)(2,1)S(1)}, bf16[8,128,1280]{2,1,0:T(8,128)(2,1)S(1)}, bf16[8,128...) fusion(bf16[10,128,1280]{2,1,0:T(8,128)(2,1)S(1)} %maximum_sele, ...), kind=kLoop, calls=%fused_computation.2 | loop fusion | bytes 34734080 | tf_op jit(solution)/shard_map/slice | solution.py:113
  77.8 0.0 slice-start
  77.8 2.3 %fusion.14 = f32[1024,320]{0,1:T(8,128)S(1)} fusion(bf16[1024,1280]{1,0:T(8,128)(2,1)S(1)} %bitcast.89, bf16[9,1280,320]{1,2,0:T(8,128)(2,1)} %param.12), kind=kOutput, calls=%fused_computation.32 | convolution fusion | flops 838860800 | bytes 4751360 | tf_op jit(solution)/shard_map/dot_general | solution.py:114
  80.1 0.0 slice-start.1
  80.2 2.3 %convolution_add_fusion.7 = f32[1024,320]{0,1:T(8,128)S(1)} fusion(f32[1024,320]{0,1:T(8,128)S(1)} %fusion.14, bf16[1024,1280]{1,0:T(8,128)(2,1)S(1)} %bitcast.88, bf16[9,1280,320]{1,2,0:T(8,128)(2,1)} %param.12), kind=kOutput, calls=%fused_computation.20 | convolution fusion | flops 839188480 | bytes 6062080 | tf_op jit(solution)/shard_map/dot_general | solution.py:114
  82.5 0.1 slice-done.1
  82.6 1.0 %convolution_add_fusion.6 = f32[1024,320]{0,1:T(8,128)S(1)} fusion(f32[1024,320]{0,1:T(8,128)S(1)} %convolution_add_fusion.7, bf16[1024,1280]{1,0:T(8,128)(2,1)S(1)} %bitcast.87, bf16[9,1280,320]{1,2,0:T(8,128)(2,1)S(1)} %bitcast.95), kind=kOutput, calls=%fused_computation.19 | convolution fusion | flops 839188480 | bytes 6062080 | tf_op jit(solution)/shard_map/dot_general | solution.py:114
  83.6 1.0 convolution_add_fusion.5
  84.7 1.0 %convolution_add_fusion.4 = f32[1024,320]{0,1:T(8,128)S(1)} fusion(f32[1024,320]{0,1:T(8,128)S(1)} %convolution_add_fusion.5, bf16[1024,1280]{1,0:T(8,128)(2,1)S(1)} %bitcast.85, bf16[9,1280,320]{1,2,0:T(8,128)(2,1)S(1)} %bitcast.95), kind=kOutput, calls=%fused_computation.17 | convolution fusion | flops 839188480 | bytes 6062080 | tf_op jit(solution)/shard_map/dot_general | solution.py:114
  85.7 1.0 %convolution_add_fusion.3 = f32[1024,320]{0,1:T(8,128)S(1)} fusion(f32[1024,320]{0,1:T(8,128)S(1)} %convolution_add_fusion.4, bf16[1024,1280]{1,0:T(8,128)(2,1)S(1)} %bitcast.84, bf16[9,1280,320]{1,2,0:T(8,128)(2,1)S(1)} %bitcast.95), kind=kOutput, calls=%fused_computation.16 | convolution fusion | flops 839188480 | bytes 6062080 | tf_op jit(solution)/shard_map/dot_general | solution.py:114
  86.8 1.0 convolution_add_fusion.2
  87.8 1.0 %convolution_add_fusion.1 = f32[1024,320]{0,1:T(8,128)S(1)} fusion(f32[1024,320]{0,1:T(8,128)S(1)} %convolution_add_fusion.2, bf16[1024,1280]{1,0:T(8,128)(2,1)S(1)} %bitcast.82, bf16[9,1280,320]{1,2,0:T(8,128)(2,1)S(1)} %bitcast.95), kind=kOutput, calls=%fused_computation.14 | convolution fusion | flops 839188480 | bytes 6062080 | tf_op jit(solution)/shard_map/dot_general | solution.py:114
  88.9 0.0 copy-start
  88.9 1.0 %fusion.2 = f32[40,8,8,128]{3,2,1,0:T(8,128)S(1)} fusion(f32[1024,320]{0,1:T(8,128)S(1)} %convolution_add_fusion.1, bf16[1024,1280]{1,0:T(8,128)(2,1)S(1)} %bitcast.81, bf16[9,1280,320]{1,2,0:T(8,128)(2,1)S(1)} %bitcast.95), kind=kOutput, calls=%fused_computation.13 | convolution fusion | flops 839188480 | bytes 6062080 | tf_op jit(solution)/shard_map/dot_general | solution.py:114
  89.9 0.0 copy-done
  90.0 0.2 fusion.5
  90.2 0.2 broadcast_in_dim.52
  90.4 1.9 %copy.47 = bf16[16,128,320]{2,0,1:T(8,128)(2,1)} copy(bf16[16,128,320]{1,2,0:T(8,128)(2,1)S(1)} %bitcast.80) | data formatting | bytes 2621440 | tf_op jit(solution)/shard_map/reshape | solution.py:118
  92.3 1.7 %broadcast_in_dim.53 = bf16[16,128,2,320]{3,0,2,1:T(8,128)(2,1)S(1)} broadcast(bf16[16,128,320]{2,0,1:T(8,128)(2,1)} %copy.47), dimensions={0,1,3} | broadcast | bytes 3932160 | tf_op jit(solution)/shard_map/broadcast_in_dim | solution.py:118
  94.0 3.1 %copy.49 = bf16[16,256,320]{1,2,0:T(8,128)(2,1)} copy(bf16[16,256,320]{2,0,1:T(8,128)(2,1)S(1)} %bitcast.79) | data formatting | bytes 5242880
  (33 shorter events, 0.3 us)
Async XLA Ops:
  7.2 4.7 %copy-start.2 = (s32[1280]{0:T(1024)S(1)}, s32[1280]{0:T(1024)}, u32[]{:S(2)}) copy-start(s32[1280]{0:T(1024)} %param.15) | copy-start | bytes 15364
  7.2 11.0 %copy-start.1 = (bf16[2,128,320]{1,2,0:T(8,128)(2,1)S(1)}, bf16[2,128,320]{1,2,0:T(8,128)(2,1)}, u32[]{:S(2)}) copy-start(bf16[2,128,320]{1,2,0:T(8,128)(2,1)} %param.17) | copy-start | bytes 491524
  7.2 30.2 %copy-start.8 = (f32[32]{0:T(128)S(1)}, f32[32]{0:T(128)}, u32[]{:S(2)}) copy-start(f32[32]{0:T(128)} %param.18) | copy-start | bytes 388
  7.2 30.2 %copy-start.6 = (f32[32]{0:T(128)S(1)}, f32[32]{0:T(128)}, u32[]{:S(2)}) copy-start(f32[32]{0:T(128)} %param.19) | copy-start | bytes 388
  7.2 30.2 %copy-start.7 = (f32[1,32]{1,0:T(1,128)S(1)}, f32[1,32]{1,0:T(1,128)}, u32[]{:S(2)}) copy-start(f32[1,32]{1,0:T(1,128)} %param.20) | copy-start | bytes 388
  7.2 30.2 %copy-start.5 = (f32[1,32]{1,0:T(1,128)S(1)}, f32[1,32]{1,0:T(1,128)}, u32[]{:S(2)}) copy-start(f32[1,32]{1,0:T(1,128)} %param.21) | copy-start | bytes 388
  7.2 42.7 %copy-start.4 = (f32[1280]{0:T(1024)S(1)}, f32[1280]{0:T(1024)}, u32[]{:S(2)}) copy-start(f32[1280]{0:T(1024)} %param.13) | copy-start | bytes 15364
  7.2 42.7 %copy-start.3 = (f32[1280]{0:T(1024)S(1)}, f32[1280]{0:T(1024)}, u32[]{:S(2)}) copy-start(f32[1280]{0:T(1024)} %param.14) | copy-start | bytes 15364
  7.2 54.3 %all-gather.2.cloned.1.call-start = ((), (), s32[]{:S(2)}) async-start(), calls=%async_computation.2 | async-start | bytes 3276800 | tf_op jit(solution)/shard_map/all_gather | solution.py:103
  12.8 9.2 %all-to-all-start = ((f32[4,1,64]{2,1,0:T(1,128)}), f32[4,1,64]{2,1,0:T(1,128)S(1)}, u32[]{:S(2)}, u32[]{:S(2)}) async-start(f32[4,1,64]{2,1,0:T(1,128)} %broadcast_in_dim.50), calls=%async_computation | async-start | bytes 4096 | tf_op jit(solution)/shard_map/all_to_all | solution.py:28
  18.2 19.1 %collective-permute-start = (bf16[1,128,320]{1,2,0:T(8,128)(2,1)S(1)}, bf16[1,128,320]{1,2,0:T(8,128)(2,1)S(1)}, u32[]{:S(2)}, u32[]{:S(2)}) collective-permute-start(bf16[1,128,320]{1,2,0:T(8,128)(2,1)S(1)} %get-tuple-element.43), channel_id=1, source_target_pairs={{0,4},{4,8},{8,12},{12,16},{16,20},{20,24},{24,28},{28,32},{32,36}... | collective-permute-start | bytes 245768 | tf_op jit(solution)/shard_map/ppermute | solution.py:48
  19.5 17.8 %collective-permute-start.1 = (bf16[1,128,320]{1,2,0:T(8,128)(2,1)S(1)}, bf16[1,128,320]{1,2,0:T(8,128)(2,1)S(1)}, u32[]{:S(2)}, u32[]{:S(2)}) collective-permute-start(bf16[1,128,320]{1,2,0:T(8,128)(2,1)S(1)} %get-tuple-element.44), channel_id=1, source_target_pairs={{4,0},{8,4},{12,8},{16,12},{20,16},{24,20},{28,24},{32,28},{36,32}... | collective-permute-start | bytes 245768 | tf_op jit(solution)/shard_map/ppermute | solution.py:51
  22.7 27.3 %all-to-all-start.1 = ((f32[64,1,64]{2,1,0:T(1,128)}), f32[64,1,64]{2,1,0:T(1,128)S(1)}, u32[]{:S(2)}, u32[]{:S(2)}) async-start(f32[64,1,64]{2,1,0:T(1,128)} %broadcast_in_dim.54), calls=%async_computation.1 | async-start | bytes 65536 | tf_op jit(solution)/shard_map/all_to_all | solution.py:28
  37.3 10.4 %collective-permute-start.2 = (bf16[1,2,128,320]{2,3,0,1:T(8,128)(2,1)S(1)}, bf16[1,2,128,320]{2,3,0,1:T(8,128)(2,1)S(1)}, u32[]{:S(2)}, u32[]{:S(2)}) collective-permute-start(bf16[1,2,128,320]{2,3,0,1:T(8,128)(2,1)S(1)} %maximum_bitcast_fusion.1), channel_id=1, source_target_pairs={{0,1},{1,0},{2,3},{3,2},{4,5},{5,4},{6,7},{7,6},{8,9},{9,8},{10,11... | collective-permute-start | bytes 491528 | tf_op jit(solution)/shard_map/ppermute | solution.py:19
  47.8 13.2 %collective-permute-start.3 = (bf16[2,2,128,320]{2,3,0,1:T(8,128)(2,1)S(1)}, bf16[2,2,128,320]{2,3,0,1:T(8,128)(2,1)S(1)}, u32[]{:S(2)}, u32[]{:S(2)}) collective-permute-start(bf16[2,2,128,320]{2,3,0,1:T(8,128)(2,1)S(1)} %pad_maximum_fusion), channel_id=1, source_target_pairs={{0,2},{1,3},{2,0},{3,1},{4,6},{5,7},{6,4},{7,5},{8,10},{9,11},{10,... | collective-permute-start | bytes 983048 | tf_op jit(solution)/shard_map/ppermute | solution.py:19
  77.8 4.7 %slice-start = ((s8[7372800]{0:T(1024)(128)(4,1)}), s8[3178496]{0:T(1024)(128)(4,1)S(1)}, s32[]{:S(2)}) async-start(s8[7372800]{0:T(1024)(128)(4,1)} %bitcast.94), calls=%async_computation.3 | async-start | bytes 6356992
  80.1 2.4 %slice-start.1 = ((s8[7372800]{0:T(1024)(128)(4,1)}), s8[4194304]{0:T(1024)(128)(4,1)S(1)}, s32[]{:S(2)}) async-start(s8[7372800]{0:T(1024)(128)(4,1)} %bitcast.94), calls=%async_computation.4 | async-start | bytes 8388608
  88.9 1.1 %copy-start = (bf16[8,128,320]{1,2,0:T(8,128)(2,1)S(1)}, bf16[8,128,320]{1,2,0:T(8,128)(2,1)}, u32[]{:S(2)}) copy-start(bf16[8,128,320]{1,2,0:T(8,128)(2,1)} %param.11) | copy-start | bytes 1966084
Sparse Core Ops, SparseCore 0:
  10.4 42.8 all-gather.1
